TPU v7x, 128 devices: a whole 4x4x4 slice. The times are simulated.
128 devices in a mesh: row: 8 (over x, core), col: 16 (over z, y).
Axes of the slice: x: 4, y: 4, z: 4, core: 2. Of those that a mesh axis runs over, the one named last changes fastest.
Arguments:
- fock_matrix: float32 [4096, 4096], P('row', 'col'), as said below
- density: float32 [4096, 4096], P('row', 'col'), as said below
- basis_gram: float32 [4096, 4096], P('row', 'col'), as said below
- error_history: float32 [6, 4096, 4096], P(None, 'row', 'col'), as said below
- fock_history: float32 [6, 4096, 4096], P(None, 'row', 'col'), may hold values from -6 to 6
Outputs:
- fock_next: float32 [4096, 4096], P('row', 'col')
- error_new: float32 [4096, 4096], P('row', 'col')
- weights: float32 [7], replicated
Inputs may be any that keep to these rules, and one draw needn't show every extreme that they name: `fock_matrix`: symmetric. `density`: symmetric. `basis_gram`: symmetric. `error_history`: each of the 6 matrices is antisymmetric.
All inputs are finite; a program needn't handle non-finite values.
Results may differ from a plain program's by a relative error of at most 0.000098.
Values sent between devices are 32-bit elements; how exact they have to be, the bound alone decides.
A program may use at most 128 MiB of HBM per device.

v0:
```python
import jax
import jax.numpy as jnp
from jax import lax
from jax.sharding import Mesh
from jax.sharding import PartitionSpec as P

ROW = ("row_0", "row_1")
COL = ("col_0", "col_1")


def from_everyone(shard, axis):
    devices = lax.axis_size(axis)
    return lax.all_to_all(
        jnp.broadcast_to(shard[None], (devices, *shard.shape)), axis, 0, 0, tiled=True
    )


def laid_out(parts, dim):
    lengths = list(parts.shape[1:])
    lengths[dim] *= parts.shape[0]
    return jnp.moveaxis(parts, 0, dim).reshape(lengths)


def gathered_by_axis(shard, axes, dim):
    far, near = axes
    parts = from_everyone(from_everyone(shard, far), near)
    return laid_out(parts.swapaxes(0, 1).reshape(-1, *shard.shape), dim)


def from_partner(value, axis, stride):
    mask = 2**stride
    pairs = [(source, source ^ mask) for source in range(lax.axis_size(axis))]
    return lax.ppermute(value, axis, pairs)


def over_copies(shard, axis):
    return from_everyone(shard, axis).sum(axis=0)


def by_axis(shard, axes):
    far, near = axes
    nearer = over_copies(shard, near)
    return over_copies(nearer, far)


def body(fock_matrix, density, basis_gram, error_history, fock_history):
    highest = lax.Precision.HIGHEST
    row_index = lax.axis_index(ROW)
    col_index = lax.axis_index(COL)
    dens_rows = lax.all_gather(density, COL, axis=1, tiled=True)
    gram_cols = gathered_by_axis(basis_gram, ("row_0", "row_1"), 0)
    middle = jnp.dot(dens_rows, gram_cols, precision=highest, preferred_element_type=jnp.float32)
    fock_rows = lax.all_gather(fock_matrix, COL, axis=1, tiled=True)
    middle_cols = gathered_by_axis(middle, ("row_0", "row_1"), 0)
    product = jnp.dot(fock_rows, middle_cols, precision=highest, preferred_element_type=jnp.float32)
    block_cols = product.shape[1]
    own_bit = col_index % 2
    upper_half = product[:block_cols]
    lower_half = product[block_cols:]
    keep_half = jnp.where(own_bit == 0, upper_half, lower_half)
    send_half = jnp.where(own_bit == 0, lower_half, upper_half)
    partner_half = from_partner(send_half, COL, 0)
    moving = jnp.where(
        own_bit == 0,
        jnp.concatenate([keep_half, partner_half], axis=1),
        jnp.concatenate([partner_half, keep_half], axis=1),
    )
    row_bits = lax.axis_size(ROW).bit_length() - 1
    for level in range(row_bits):
        row_bit = row_index // 2**level % 2
        col_bit = col_index // 2 ** (level + 1) % 2
        passing = from_partner(moving, ROW, level)
        arrived = from_partner(passing, COL, level + 1)
        moving = jnp.where(row_bit != col_bit, arrived, moving)
    flipped = moving.T
    error_new = product - flipped
    stacked = jnp.concatenate([error_history, error_new[None]], axis=0)
    gram_local = jnp.einsum("kij,lij->kl", stacked, stacked, precision=highest)
    gram = by_axis(gram_local, ("row_0", ("row_1", "col_0", "col_1")))
    size = gram.shape[0]
    factor = jnp.linalg.cholesky(gram)
    forward = []
    for index in range(size):
        total = jnp.float32(1.0)
        for inner in range(index):
            total = total - factor[index, inner] * forward[inner]
        forward.append(total / factor[index, index])
    backward = [None] * size
    for index in range(size - 1, -1, -1):
        total = forward[index]
        for inner in range(index + 1, size):
            total = total - factor[inner, index] * backward[inner]
        backward[index] = total / factor[index, index]
    solved = jnp.stack(backward)
    weights = solved / jnp.sum(solved)
    history_count = fock_history.shape[0]
    fock_next = (
        jnp.einsum("k,kij->ij", weights[:history_count], fock_history, precision=highest)
        + weights[history_count] * fock_matrix
    )
    return (fock_next, error_new, weights)


def solution(mesh):
    split = Mesh(mesh.devices.reshape(4, 2, 4, 4), ("row_0", "row_1", "col_0", "col_1"))
    placed = (P(ROW, COL), P(ROW, COL), P(ROW, COL), P(None, ROW, COL), P(None, ROW, COL))
    return jax.shard_map(
        body,
        mesh=split,
        in_specs=placed,
        out_specs=(P(ROW, COL), P(ROW, COL), P()),
        check_vma=False,
    )
```

profile of v0, /device:TPU:0, one launch (start us, length us, event | category | flops | bytes accessed | tf_op | source)
XLA Modules:
  0.0 365.2 jit_solution(14596943696388433436)
XLA Ops:
  9.9 30.5 %all_to_all.30 = f32[4,512,256]{2,1,0:T(8,128)S(1)} all-to-all(f32[4,512,256]{2,1,0:T(8,128)S(1)} %broadcast_in_dim.15), channel_id=1, replica_groups=mesh['row_0'=4,'row_1'=2,'col_0'=4,'col_1'=4] {'row_0'}, dimensions={0} | all-to-all | bytes 4194304 | tf_op jit(solution)/shard_map/all_to_all | solution.py:13
  40.8 7.1 %all_to_all.31 = f32[2,4,512,256]{3,2,1,0:T(8,128)S(1)} all-to-all(f32[2,4,512,256]{3,2,1,0:T(8,128)S(1)} %broadcast_in_dim.16), channel_id=1, replica_groups=mesh['row_0'=4,'row_1'=2,'col_0'=4,'col_1'=4] {'row_1'}, dimensions={0} | all-to-all | bytes 8388608 | tf_op jit(solution)/shard_map/all_to_all | solution.py:13
  50.1 39.9 %all-gather.3.cloned.1.call-done = f32[512,4096]{1,0:T(8,128)} async-done(((f32[512,256]{1,0:T(8,128)}), f32[512,4096]{1,0:T(8,128)}) %all-gather.3.cloned.1.call-update) | async-done | bytes 8388624 | tf_op jit(solution)/shard_map/all_gather | solution.py:50
  90.0 9.8 %fusion.16 = f32[512,256]{1,0:T(8,128)S(1)} fusion(f32[512,4096]{1,0:T(8,128)} %all-gather.3.cloned.1.call-done, f32[4096,256]{1,0:T(8,128)} %bitcast.63), kind=kOutput, calls=%fused_computation.29 | convolution fusion | flops 6442450944 | bytes 13107200 | tf_op jit(solution)/shard_map/dot_general | solution.py:52
  101.3 4.5 %all-to-all-start.2 = ((f32[4,512,256]{2,1,0:T(8,128)}), f32[4,512,256]{2,1,0:T(8,128)}, u32[]{:S(2)}, u32[]{:S(2)}) async-start(f32[4,512,256]{2,1,0:T(8,128)} %broadcast_in_dim.17), calls=%async_computation.2 | async-start | bytes 4194304 | tf_op jit(solution)/shard_map/all_to_all | solution.py:13
  105.8 25.3 %all-to-all-done.2 = f32[4,512,256]{2,1,0:T(8,128)} async-done(((f32[4,512,256]{2,1,0:T(8,128)}), f32[4,512,256]{2,1,0:T(8,128)}, u32[]{:S(2)}, u32[]{:S(2)}) %all-to-all-start.2) | async-done | bytes 2097184 | tf_op jit(solution)/shard_map/all_to_all | solution.py:13
  133.1 7.1 %all_to_all.32 = f32[2,4,512,256]{3,2,1,0:T(8,128)S(1)} all-to-all(f32[2,4,512,256]{3,2,1,0:T(8,128)S(1)} %broadcast_in_dim.18), channel_id=1, replica_groups=mesh['row_0'=4,'row_1'=2,'col_0'=4,'col_1'=4] {'row_1'}, dimensions={0} | all-to-all | bytes 8388608 | tf_op jit(solution)/shard_map/all_to_all | solution.py:13
  140.2 2.2 copy.37
  142.5 26.3 %all-gather.5.cloned.1.call-done = f32[512,4096]{1,0:T(8,128)} async-done(((f32[512,256]{1,0:T(8,128)}), f32[512,4096]{1,0:T(8,128)}) %all-gather.5.cloned.1.call-update) | async-done | bytes 8388624 | tf_op jit(solution)/shard_map/all_gather | solution.py:53
  168.8 16.5 %convolution_bitcast_fusion = f32[512,256]{0,1:T(8,128)S(1)} fusion(f32[4096,256]{1,0:T(8,128)} %bitcast.62, f32[512,4096]{1,0:T(8,128)} %all-gather.5.cloned.1.call-done), kind=kOutput, calls=%fused_computation.6 | convolution fusion | flops 6442450944 | bytes 13107200 | tf_op jit(solution)/shard_map/dot_general | solution.py:55
  192.0 5.5 %collective-permute-done = f32[256,256]{1,0:T(8,128)S(1)} collective-permute-done((f32[256,256]{1,0:T(8,128)S(1)}, f32[256,256]{1,0:T(8,128)S(1)}, u32[]{:S(2)}, u32[]{:S(2)}) %collective-permute-start) | collective-permute-done | bytes 262176 | tf_op jit(solution)/shard_map/ppermute | solution.py:33
  202.5 13.7 %collective-permute-done.2 = f32[256,512]{1,0:T(8,128)} collective-permute-done((f32[256,512]{1,0:T(8,128)}, f32[256,512]{1,0:T(8,128)}, u32[]{:S(2)}, u32[]{:S(2)}) %collective-permute-start.2) | collective-permute-done | bytes 524320 | tf_op jit(solution)/shard_map/ppermute | solution.py:33
  219.6 11.7 %collective-permute-done.3 = f32[256,512]{1,0:T(8,128)} collective-permute-done((f32[256,512]{1,0:T(8,128)S(1)}, f32[256,512]{1,0:T(8,128)}, u32[]{:S(2)}, u32[]{:S(2)}) %collective-permute-start.3) | collective-permute-done | bytes 524320 | tf_op jit(solution)/shard_map/ppermute | solution.py:33
  232.5 11.4 %collective-permute-done.4 = f32[256,512]{1,0:T(8,128)} collective-permute-done((f32[256,512]{1,0:T(8,128)}, f32[256,512]{1,0:T(8,128)}, u32[]{:S(2)}, u32[]{:S(2)}) %collective-permute-start.4) | collective-permute-done | bytes 524320 | tf_op jit(solution)/shard_map/ppermute | solution.py:33
  245.8 3.0 collective-permute-start.5
  248.8 10.0 %collective-permute-done.5 = f32[256,512]{1,0:T(8,128)} collective-permute-done((f32[256,512]{1,0:T(8,128)S(1)}, f32[256,512]{1,0:T(8,128)}, u32[]{:S(2)}, u32[]{:S(2)}) %collective-permute-start.5) | collective-permute-done | bytes 524320 | tf_op jit(solution)/shard_map/ppermute | solution.py:33
  258.8 2.4 collective-permute-start.6
  261.2 5.7 %copy.40 = f32[6,512,256]{2,0,1:T(8,128)} copy(f32[6,512,256]{2,1,0:T(8,128)} %param.8) | data formatting | bytes 6291456 | tf_op args[3]
  267.0 4.2 %collective-permute-done.6 = f32[256,512]{1,0:T(8,128)} collective-permute-done((f32[256,512]{1,0:T(8,128)}, f32[256,512]{1,0:T(8,128)}, u32[]{:S(2)}, u32[]{:S(2)}) %collective-permute-start.6) | collective-permute-done | bytes 524320 | tf_op jit(solution)/shard_map/ppermute | solution.py:33
  275.2 13.4 %fusion.6 = f32[7,7]{1,0:T(8,128)S(1)} fusion(f32[1,512,256]{2,0,1:T(1,128)} %copy.41, f32[6,512,256]{2,0,1:T(8,128)} %copy.40), kind=kOutput, calls=%fused_computation.7 | convolution fusion | flops 77987840 | bytes 3670212 | tf_op jit(solution)/shard_map/kij,lij->kl/dot_general | solution.py:78
  288.7 12.8 %all_to_all.33 = f32[32,7,7]{2,1,0:T(8,128)S(1)} all-to-all(f32[32,7,7]{2,1,0:T(8,128)S(1)} %broadcast_in_dim.20), channel_id=1, replica_groups=mesh['row_0'=4,'row_1'=2,'col_0'=4,'col_1'=4] {'row_1','col_0','col_1'}, dimensions={0} | all-to-all | bytes 12544 | tf_op jit(solution)/shard_map/all_to_all | solution.py:13
  302.1 4.2 %all-to-all-start.5 = ((f32[4,7,7]{2,1,0:T(8,128)}), f32[4,7,7]{2,1,0:T(8,128)S(1)}, u32[]{:S(2)}, u32[]{:S(2)}) async-start(f32[4,7,7]{2,1,0:T(8,128)} %broadcast_in_dim.21), calls=%async_computation.5 | async-start | bytes 32768 | tf_op jit(solution)/shard_map/all_to_all | solution.py:13
  308.4 3.3 all-to-all-done.5
  351.7 5.2 %fusion.4 = f32[1,512,256]{2,0,1:T(1,128)S(1)} fusion(f32[6,512,256]{2,1,0:T(8,128)S(1)} %copy-done, f32[7]{0:T(128)S(1)} %broadcast_divide_fusion), kind=kOutput, calls=%fused_computation.4 | convolution fusion | flops 9437184 | bytes 3670044 | tf_op jit(solution)/shard_map/k,kij->ij/dot_general | solution.py:98
  (55 shorter events, 39.4 us)
Async XLA Ops:
  7.2 344.5 %copy-start = (f32[6,512,256]{2,1,0:T(8,128)S(1)}, f32[6,512,256]{2,1,0:T(8,128)}, u32[]{:S(2)}) copy-start(f32[6,512,256]{2,1,0:T(8,128)} %param.9) | copy-start | bytes 9437188
  7.2 82.8 %all-gather.3.cloned.1.call-start = ((), (), s32[]{:S(2)}) async-start(), calls=%async_computation.6 | async-start | bytes 8912896 | tf_op jit(solution)/shard_map/all_gather | solution.py:50
  7.9 160.9 %all-gather.5.cloned.1.call-start = ((), (), s32[]{:S(2)}) async-start(), calls=%async_computation.7 | async-start | bytes 8912896 | tf_op jit(solution)/shard_map/all_gather | solution.py:53
  101.3 29.8 %all-to-all-start.2 = ((f32[4,512,256]{2,1,0:T(8,128)}), f32[4,512,256]{2,1,0:T(8,128)}, u32[]{:S(2)}, u32[]{:S(2)}) async-start(f32[4,512,256]{2,1,0:T(8,128)} %broadcast_in_dim.17), calls=%async_computation.2 | async-start | bytes 4194304 | tf_op jit(solution)/shard_map/all_to_all | solution.py:13
  185.3 0.8 copy-start.1
  190.7 6.8 %collective-permute-start = (f32[256,256]{1,0:T(8,128)S(1)}, f32[256,256]{1,0:T(8,128)S(1)}, u32[]{:S(2)}, u32[]{:S(2)}) collective-permute-start(f32[256,256]{1,0:T(8,128)S(1)} %get-tuple-element.19), channel_id=1, source_target_pairs={{0,1},{1,0},{2,3},{3,2},{4,5},{5,4},{6,7},{7,6},{8,9},{9,8},{10,11... | collective-permute-start | bytes 786440 | tf_op jit(solution)/shard_map/ppermute | solution.py:33
  197.5 0.8 copy-start.5
  198.3 2.0 collective-permute-start.1
  200.4 15.8 %collective-permute-start.2 = (f32[256,512]{1,0:T(8,128)}, f32[256,512]{1,0:T(8,128)}, u32[]{:S(2)}, u32[]{:S(2)}) collective-permute-start(f32[256,512]{1,0:T(8,128)} %collective-permute-done.1), channel_id=1, source_target_pairs={{0,2},{1,3},{2,0},{3,1},{4,6},{5,7},{6,4},{7,5},{8,10},{9,11},{10,... | collective-permute-start | bytes 1572872 | tf_op jit(solution)/shard_map/ppermute | solution.py:33
  217.3 0.8 copy-start.4
  218.1 13.2 %collective-permute-start.3 = (f32[256,512]{1,0:T(8,128)S(1)}, f32[256,512]{1,0:T(8,128)}, u32[]{:S(2)}, u32[]{:S(2)}) collective-permute-start(f32[256,512]{1,0:T(8,128)S(1)} %broadcast_select_fusion), channel_id=1, source_target_pairs={{0,32},{16,48},{32,0},{48,16},{64,96},{80,112},{96,64},{112,80},{1... | collective-permute-start | bytes 1572872 | tf_op jit(solution)/shard_map/ppermute | solution.py:33
  231.3 12.6 %collective-permute-start.4 = (f32[256,512]{1,0:T(8,128)}, f32[256,512]{1,0:T(8,128)}, u32[]{:S(2)}, u32[]{:S(2)}) collective-permute-start(f32[256,512]{1,0:T(8,128)} %collective-permute-done.3), channel_id=1, source_target_pairs={{0,4},{1,5},{2,6},{3,7},{4,0},{5,1},{6,2},{7,3},{8,12},{9,13},{10,... | collective-permute-start | bytes 1572872 | tf_op jit(solution)/shard_map/ppermute | solution.py:33
  245.0 0.8 copy-start.2
  245.8 13.0 %collective-permute-start.5 = (f32[256,512]{1,0:T(8,128)S(1)}, f32[256,512]{1,0:T(8,128)}, u32[]{:S(2)}, u32[]{:S(2)}) collective-permute-start(f32[256,512]{1,0:T(8,128)S(1)} %broadcast_select_fusion.1), channel_id=1, source_target_pairs={{0,64},{16,80},{32,96},{48,112},{64,0},{80,16},{96,32},{112,48},{1... | collective-permute-start | bytes 1572872 | tf_op jit(solution)/shard_map/ppermute | solution.py:33
  258.8 12.4 %collective-permute-start.6 = (f32[256,512]{1,0:T(8,128)}, f32[256,512]{1,0:T(8,128)}, u32[]{:S(2)}, u32[]{:S(2)}) collective-permute-start(f32[256,512]{1,0:T(8,128)} %collective-permute-done.5), channel_id=1, source_target_pairs={{0,8},{1,9},{2,10},{3,11},{4,12},{5,13},{6,14},{7,15},{8,0},{9,1},... | collective-permute-start | bytes 1572872 | tf_op jit(solution)/shard_map/ppermute | solution.py:33
  302.1 9.6 %all-to-all-start.5 = ((f32[4,7,7]{2,1,0:T(8,128)}), f32[4,7,7]{2,1,0:T(8,128)S(1)}, u32[]{:S(2)}, u32[]{:S(2)}) async-start(f32[4,7,7]{2,1,0:T(8,128)} %broadcast_in_dim.21), calls=%async_computation.5 | async-start | bytes 32768 | tf_op jit(solution)/shard_map/all_to_all | solution.py:13
  351.1 5.8 %copy-start.3 = (f32[512,256]{1,0:T(8,128)S(1)}, f32[512,256]{1,0:T(8,128)}, u32[]{:S(2)}) copy-start(f32[512,256]{1,0:T(8,128)} %param.5) | copy-start | bytes 1572868
  351.1 7.3 %copy-start.6 = (f32[7]{0:T(128)}, f32[7]{0:T(128)S(1)}, u32[]{:S(2)}) copy-start(f32[7]{0:T(128)S(1)} %broadcast_divide_fusion) | copy-start | bytes 88
Sparse Core Ops, SparseCore 0:
  10.1 79.8 all-gather.2
  92.1 76.6 all-gather.4
where the time goes:
time: 367 us; the launch traced here: 365 us
  waiting for transfers between devices  155 us (42%)
  blocking collectives  57.6 us (16%)
  between operations  50 us (14%)
  matrix products  44.8 us (12%)
  local copies, waits for them, and re-layouts  28.9 us (8%)
  starting transfers between devices  20.3 us (6%)
  other arithmetic  8.92 us (2%)
    ppermute x7, waiting for transfers between devices, from_partner(): return lax.ppermute(value, axis, pairs)  58.6 us
    all_to_all x4, blocking collectives, from_everyone(): lax.all_to_all(jnp.broadcast_to(shard[None], (devices, *shard.shape)), ax...  57.6 us
    all_gather x1, waiting for transfers between devices, body(): dens_rows = lax.all_gather(density, COL, axis=1, tiled=True)  39.9 us
    all_to_all x2, waiting for transfers between devices, from_everyone(): lax.all_to_all(jnp.broadcast_to(shard[None], (devices, *shard.shape)), ax...  28.6 us
    all_gather x1, waiting for transfers between devices, body(): fock_rows = lax.all_gather(fock_matrix, COL, axis=1, tiled=True)  26.3 us
    dot_general x1, matrix products, body(): jnp.dot(fock_rows, middle_cols, precision=highest, preferred_element_type...  16.5 us
    unnamed x18, local copies, waits for them, and re-layouts  13.8 us
    dot_general x1, matrix products, body(): gram_local = jnp.einsum('kij,lij->kl', stacked, stacked, precision=highest)  13.4 us
  transfers between devices with their start and end apart: 11, of which 11 were waited for; matrix products, arithmetic and copies ran while one was open for 7% of the time, Pallas kernels for 0%

commit v1 on v0

--- a/solution.py
+++ b/solution.py
@@ -50,7 +50,9 @@
     dens_rows = lax.all_gather(density, COL, axis=1, tiled=True)
     gram_cols = gathered_by_axis(basis_gram, ("row_0", "row_1"), 0)
     middle = jnp.dot(dens_rows, gram_cols, precision=highest, preferred_element_type=jnp.float32)
-    fock_rows = lax.all_gather(fock_matrix, COL, axis=1, tiled=True)
+    fock_rows = jnp.concatenate(
+        lax.all_to_all(jnp.stack([fock_matrix] * lax.axis_size(COL)), COL, 0, 0), axis=1
+    )
     middle_cols = gathered_by_axis(middle, ("row_0", "row_1"), 0)
     product = jnp.dot(fock_rows, middle_cols, precision=highest, preferred_element_type=jnp.float32)
     block_cols = product.shape[1]

time: 367 us -> 467 us (1.27)
  waiting for transfers between devices: 155 us -> 254 us
  local copies, waits for them, and re-layouts: 28.9 us -> 37.6 us
  matrix products: 44.8 us -> 38.5 us
    all_to_all x0 -> x1, waiting for transfers between devices: none -> 121 us  [body(): lax.all_to_all(jnp.stack([fock_matrix] * lax.axis_size(COL)), COL, 0, 0)]
    all_gather x1 -> x0, waiting for transfers between devices: 26.3 us -> none  [body(): fock_rows = lax.all_gather(fock_matrix, COL, axis=1, tiled=True)]
    ppermute x7, waiting for transfers between devices: 58.6 us -> 65.6 us  [from_partner(): return lax.ppermute(value, axis, pairs)]
    ppermute x7, starting transfers between devices: 11.4 us -> 4.96 us  [from_partner(): return lax.ppermute(value, axis, pairs)]
    dot_general x1, matrix products: 16.5 us -> 10.2 us  [body(): jnp.dot(fock_rows, middle_cols, precision=highest, preferred_element_type...]
    all_to_all x0 -> x1, starting transfers between devices: none -> 5 us  [body(): lax.all_to_all(jnp.stack([fock_matrix] * lax.axis_size(COL)), COL, 0, 0)]
    unnamed x18 -> x21, local copies, waits for them, and re-layouts: 13.8 us -> 15.9 us
  transfers between devices with their start and end apart: 11 -> 11, of which waited for: 11 -> 11; matrix products, arithmetic and copies ran while one was open for 7% -> 4% of each run, Pallas kernels for 0% -> 0%
where the time goes in v1:
time: 467 us; the launch traced here: 465 us
  waiting for transfers between devices  254 us (54%)
  blocking collectives  58.6 us (13%)
  between operations  50 us (11%)
  matrix products  38.5 us (8%)
  local copies, waits for them, and re-layouts  37.6 us (8%)
  starting transfers between devices  17.9 us (4%)
  other arithmetic  8.92 us (2%)
    all_to_all x1, waiting for transfers between devices, body(): lax.all_to_all(jnp.stack([fock_matrix] * lax.axis_size(COL)), COL, 0, 0)  121 us
    ppermute x7, waiting for transfers between devices, from_partner(): return lax.ppermute(value, axis, pairs)  65.6 us
    all_to_all x4, blocking collectives, from_everyone(): lax.all_to_all(jnp.broadcast_to(shard[None], (devices, *shard.shape)), ax...  58.6 us
    all_gather x1, waiting for transfers between devices, body(): dens_rows = lax.all_gather(density, COL, axis=1, tiled=True)  40.4 us
    all_to_all x2, waiting for transfers between devices, from_everyone(): lax.all_to_all(jnp.broadcast_to(shard[None], (devices, *shard.shape)), ax...  26.3 us
    unnamed x21, local copies, waits for them, and re-layouts  15.9 us
    dot_general x1, matrix products, body(): gram_local = jnp.einsum('kij,lij->kl', stacked, stacked, precision=highest)  13.4 us
    dot_general x1, matrix products, body(): jnp.dot(fock_rows, middle_cols, precision=highest, preferred_element_type...  10.2 us
  transfers between devices with their start and end apart: 11, of which 11 were waited for; matrix products, arithmetic and copies ran while one was open for 4% of the time, Pallas kernels for 0%

profile of v1, /device:TPU:0, one launch (start us, length us, event | category | flops | bytes accessed | tf_op | source)
XLA Modules:
  0.0 465.5 jit_solution(4607002317429962753)
XLA Ops:
  9.3 30.5 %all_to_all.35 = f32[4,512,256]{2,1,0:T(8,128)S(1)} all-to-all(f32[4,512,256]{2,1,0:T(8,128)S(1)} %broadcast_in_dim.15), channel_id=1, replica_groups=mesh['row_0'=4,'row_1'=2,'col_0'=4,'col_1'=4] {'row_0'}, dimensions={0} | all-to-all | bytes 4194304 | tf_op jit(solution)/shard_map/all_to_all | solution.py:13
  40.2 7.1 %all_to_all.36 = f32[2,4,512,256]{3,2,1,0:T(8,128)S(1)} all-to-all(f32[2,4,512,256]{3,2,1,0:T(8,128)S(1)} %broadcast_in_dim.16), channel_id=1, replica_groups=mesh['row_0'=4,'row_1'=2,'col_0'=4,'col_1'=4] {'row_1'}, dimensions={0} | all-to-all | bytes 8388608 | tf_op jit(solution)/shard_map/all_to_all | solution.py:13
  49.6 40.4 %all-gather.2.cloned.1.call-done = f32[512,4096]{1,0:T(8,128)} async-done(((f32[512,256]{1,0:T(8,128)}), f32[512,4096]{1,0:T(8,128)}) %all-gather.2.cloned.1.call-update) | async-done | bytes 8388624 | tf_op jit(solution)/shard_map/all_gather | solution.py:50
  90.0 9.8 %fusion.16 = f32[512,256]{1,0:T(8,128)S(1)} fusion(f32[512,4096]{1,0:T(8,128)} %all-gather.2.cloned.1.call-done, f32[4096,256]{1,0:T(8,128)} %bitcast.66), kind=kOutput, calls=%fused_computation.29 | convolution fusion | flops 6442450944 | bytes 13107200 | tf_op jit(solution)/shard_map/dot_general | solution.py:52
  101.3 4.4 all-to-all-start.2
  107.8 23.3 %all-to-all-done.2 = f32[4,512,256]{2,1,0:T(8,128)} async-done(((f32[4,512,256]{2,1,0:T(8,128)}), f32[4,512,256]{2,1,0:T(8,128)}, u32[]{:S(2)}, u32[]{:S(2)}) %all-to-all-start.2) | async-done | bytes 2097184 | tf_op jit(solution)/shard_map/all_to_all | solution.py:13
  133.0 8.3 %all_to_all.37 = f32[2,4,512,256]{3,2,1,0:T(8,128)} all-to-all(f32[2,4,512,256]{3,2,1,0:T(8,128)S(1)} %broadcast_in_dim.18), channel_id=1, replica_groups=mesh['row_0'=4,'row_1'=2,'col_0'=4,'col_1'=4] {'row_1'}, dimensions={0} | all-to-all | bytes 8388608 | tf_op jit(solution)/shard_map/all_to_all | solution.py:13
  141.3 4.3 stack.18
  145.6 5.0 %all-to-all-start.4 = ((f32[16,512,256]{1,2,0:T(8,128)}), f32[16,512,256]{1,2,0:T(8,128)}, u32[]{:S(2)}, u32[]{:S(2)}) async-start(f32[16,512,256]{1,2,0:T(8,128)} %stack.18), calls=%async_computation.4 | async-start | bytes 16777216 | tf_op jit(solution)/shard_map/all_to_all | solution.py:54
  150.6 4.5 copy.40
  155.1 120.8 %all-to-all-done.4 = f32[16,512,256]{1,2,0:T(8,128)} async-done(((f32[16,512,256]{1,2,0:T(8,128)}), f32[16,512,256]{1,2,0:T(8,128)}, u32[]{:S(2)}, u32[]{:S(2)}) %all-to-all-start.4) | async-done | bytes 8388640 | tf_op jit(solution)/shard_map/all_to_all | solution.py:54
  275.9 10.2 %convolution_bitcast_fusion = f32[512,256]{0,1:T(8,128)S(1)} fusion(f32[4096,256]{1,0:T(8,128)} %bitcast.65, f32[512,4096]{0,1:T(8,128)} %bitcast.5), kind=kOutput, calls=%fused_computation.6 | convolution fusion | flops 6442450944 | bytes 13107200 | tf_op jit(solution)/shard_map/dot_general | solution.py:57
  291.7 7.2 %collective-permute-done = f32[256,256]{1,0:T(8,128)S(1)} collective-permute-done((f32[256,256]{1,0:T(8,128)S(1)}, f32[256,256]{1,0:T(8,128)S(1)}, u32[]{:S(2)}, u32[]{:S(2)}) %collective-permute-start) | collective-permute-done | bytes 262176 | tf_op jit(solution)/shard_map/ppermute | solution.py:33
  302.5 15.1 %collective-permute-done.2 = f32[256,512]{1,0:T(8,128)} collective-permute-done((f32[256,512]{1,0:T(8,128)}, f32[256,512]{1,0:T(8,128)}, u32[]{:S(2)}, u32[]{:S(2)}) %collective-permute-start.2) | collective-permute-done | bytes 524320 | tf_op jit(solution)/shard_map/ppermute | solution.py:33
  320.1 12.6 %collective-permute-done.3 = f32[256,512]{1,0:T(8,128)} collective-permute-done((f32[256,512]{1,0:T(8,128)S(1)}, f32[256,512]{1,0:T(8,128)}, u32[]{:S(2)}, u32[]{:S(2)}) %collective-permute-start.3) | collective-permute-done | bytes 524320 | tf_op jit(solution)/shard_map/ppermute | solution.py:33
  333.3 12.0 %collective-permute-done.4 = f32[256,512]{1,0:T(8,128)} collective-permute-done((f32[256,512]{1,0:T(8,128)}, f32[256,512]{1,0:T(8,128)}, u32[]{:S(2)}, u32[]{:S(2)}) %collective-permute-start.4) | collective-permute-done | bytes 524320 | tf_op jit(solution)/shard_map/ppermute | solution.py:33
  348.4 11.8 %collective-permute-done.5 = f32[256,512]{1,0:T(8,128)} collective-permute-done((f32[256,512]{1,0:T(8,128)S(1)}, f32[256,512]{1,0:T(8,128)}, u32[]{:S(2)}, u32[]{:S(2)}) %collective-permute-start.5) | collective-permute-done | bytes 524320 | tf_op jit(solution)/shard_map/ppermute | solution.py:33
  362.1 5.7 %copy.44 = f32[6,512,256]{2,0,1:T(8,128)} copy(f32[6,512,256]{2,1,0:T(8,128)} %param.8) | data formatting | bytes 6291456 | tf_op args[3]
  367.8 4.8 %collective-permute-done.6 = f32[256,512]{1,0:T(8,128)} collective-permute-done((f32[256,512]{1,0:T(8,128)}, f32[256,512]{1,0:T(8,128)}, u32[]{:S(2)}, u32[]{:S(2)}) %collective-permute-start.6) | collective-permute-done | bytes 524320 | tf_op jit(solution)/shard_map/ppermute | solution.py:33
  376.6 13.4 %fusion.6 = f32[7,7]{1,0:T(8,128)S(1)} fusion(f32[1,512,256]{2,0,1:T(1,128)} %copy.45, f32[6,512,256]{2,0,1:T(8,128)} %copy.44), kind=kOutput, calls=%fused_computation.7 | convolution fusion | flops 77987840 | bytes 3670212 | tf_op jit(solution)/shard_map/kij,lij->kl/dot_general | solution.py:80
  390.1 12.7 %all_to_all.38 = f32[32,7,7]{2,1,0:T(8,128)S(1)} all-to-all(f32[32,7,7]{2,1,0:T(8,128)S(1)} %broadcast_in_dim.20), channel_id=1, replica_groups=mesh['row_0'=4,'row_1'=2,'col_0'=4,'col_1'=4] {'row_1','col_0','col_1'}, dimensions={0} | all-to-all | bytes 12544 | tf_op jit(solution)/shard_map/all_to_all | solution.py:13
  403.4 3.5 all-to-all-start.6
  408.9 3.1 all-to-all-done.6
  452.0 5.2 %fusion.4 = f32[1,512,256]{2,0,1:T(1,128)S(1)} fusion(f32[6,512,256]{2,1,0:T(8,128)S(1)} %copy-done, f32[7]{0:T(128)S(1)} %broadcast_divide_fusion), kind=kOutput, calls=%fused_computation.4 | convolution fusion | flops 9437184 | bytes 3670044 | tf_op jit(solution)/shard_map/k,kij->ij/dot_general | solution.py:100
  (58 shorter events, 39.7 us)
Async XLA Ops:
  7.2 444.8 %copy-start = (f32[6,512,256]{2,1,0:T(8,128)S(1)}, f32[6,512,256]{2,1,0:T(8,128)}, u32[]{:S(2)}) copy-start(f32[6,512,256]{2,1,0:T(8,128)} %param.9) | copy-start | bytes 9437188
  7.2 82.8 %all-gather.2.cloned.1.call-start = ((), (), s32[]{:S(2)}) async-start(), calls=%async_computation.7 | async-start | bytes 8912896 | tf_op jit(solution)/shard_map/all_gather | solution.py:50
  101.3 29.8 %all-to-all-start.2 = ((f32[4,512,256]{2,1,0:T(8,128)}), f32[4,512,256]{2,1,0:T(8,128)}, u32[]{:S(2)}, u32[]{:S(2)}) async-start(f32[4,512,256]{2,1,0:T(8,128)} %broadcast_in_dim.17), calls=%async_computation.2 | async-start | bytes 4194304 | tf_op jit(solution)/shard_map/all_to_all | solution.py:13
  133.0 8.3 %copy-start.3 = (f32[512,256]{0,1:T(8,128)S(1)}, f32[512,256]{0,1:T(8,128)}, u32[]{:S(2)}) copy-start(f32[512,256]{0,1:T(8,128)} %copy.41) | copy-start | bytes 1572868
  145.6 130.3 %all-to-all-start.4 = ((f32[16,512,256]{1,2,0:T(8,128)}), f32[16,512,256]{1,2,0:T(8,128)}, u32[]{:S(2)}, u32[]{:S(2)}) async-start(f32[16,512,256]{1,2,0:T(8,128)} %stack.18), calls=%async_computation.4 | async-start | bytes 16777216 | tf_op jit(solution)/shard_map/all_to_all | solution.py:54
  286.1 0.8 copy-start.1
  291.6 7.3 %collective-permute-start = (f32[256,256]{1,0:T(8,128)S(1)}, f32[256,256]{1,0:T(8,128)S(1)}, u32[]{:S(2)}, u32[]{:S(2)}) collective-permute-start(f32[256,256]{1,0:T(8,128)S(1)} %get-tuple-element.19), channel_id=1, source_target_pairs={{0,1},{1,0},{2,3},{3,2},{4,5},{5,4},{6,7},{7,6},{8,9},{9,8},{10,11... | collective-permute-start | bytes 786440 | tf_op jit(solution)/shard_map/ppermute | solution.py:33
  298.9 0.8 copy-start.6
  299.7 2.0 collective-permute-start.1
  301.8 15.8 %collective-permute-start.2 = (f32[256,512]{1,0:T(8,128)}, f32[256,512]{1,0:T(8,128)}, u32[]{:S(2)}, u32[]{:S(2)}) collective-permute-start(f32[256,512]{1,0:T(8,128)} %collective-permute-done.1), channel_id=1, source_target_pairs={{0,2},{1,3},{2,0},{3,1},{4,6},{5,7},{6,4},{7,5},{8,10},{9,11},{10,... | collective-permute-start | bytes 1572872 | tf_op jit(solution)/shard_map/ppermute | solution.py:33
  318.7 0.8 copy-start.5
  319.5 13.2 %collective-permute-start.3 = (f32[256,512]{1,0:T(8,128)S(1)}, f32[256,512]{1,0:T(8,128)}, u32[]{:S(2)}, u32[]{:S(2)}) collective-permute-start(f32[256,512]{1,0:T(8,128)S(1)} %broadcast_select_fusion), channel_id=1, source_target_pairs={{0,32},{16,48},{32,0},{48,16},{64,96},{80,112},{96,64},{112,80},{1... | collective-permute-start | bytes 1572872 | tf_op jit(solution)/shard_map/ppermute | solution.py:33
  332.7 12.6 %collective-permute-start.4 = (f32[256,512]{1,0:T(8,128)}, f32[256,512]{1,0:T(8,128)}, u32[]{:S(2)}, u32[]{:S(2)}) collective-permute-start(f32[256,512]{1,0:T(8,128)} %collective-permute-done.3), channel_id=1, source_target_pairs={{0,4},{1,5},{2,6},{3,7},{4,0},{5,1},{6,2},{7,3},{8,12},{9,13},{10,... | collective-permute-start | bytes 1572872 | tf_op jit(solution)/shard_map/ppermute | solution.py:33
  346.4 0.8 copy-start.2
  347.2 13.0 %collective-permute-start.5 = (f32[256,512]{1,0:T(8,128)S(1)}, f32[256,512]{1,0:T(8,128)}, u32[]{:S(2)}, u32[]{:S(2)}) collective-permute-start(f32[256,512]{1,0:T(8,128)S(1)} %broadcast_select_fusion.1), channel_id=1, source_target_pairs={{0,64},{16,80},{32,96},{48,112},{64,0},{80,16},{96,32},{112,48},{1... | collective-permute-start | bytes 1572872 | tf_op jit(solution)/shard_map/ppermute | solution.py:33
  360.2 12.4 %collective-permute-start.6 = (f32[256,512]{1,0:T(8,128)}, f32[256,512]{1,0:T(8,128)}, u32[]{:S(2)}, u32[]{:S(2)}) collective-permute-start(f32[256,512]{1,0:T(8,128)} %collective-permute-done.5), channel_id=1, source_target_pairs={{0,8},{1,9},{2,10},{3,11},{4,12},{5,13},{6,14},{7,15},{8,0},{9,1},... | collective-permute-start | bytes 1572872 | tf_op jit(solution)/shard_map/ppermute | solution.py:33
  403.4 8.6 %all-to-all-start.6 = ((f32[4,7,7]{2,1,0:T(8,128)}), f32[4,7,7]{2,1,0:T(8,128)S(1)}, u32[]{:S(2)}, u32[]{:S(2)}) async-start(f32[4,7,7]{2,1,0:T(8,128)} %broadcast_in_dim.21), calls=%async_computation.6 | async-start | bytes 32768 | tf_op jit(solution)/shard_map/all_to_all | solution.py:13
  451.3 5.8 %copy-start.4 = (f32[512,256]{1,0:T(8,128)S(1)}, f32[512,256]{1,0:T(8,128)}, u32[]{:S(2)}) copy-start(f32[512,256]{1,0:T(8,128)} %param.5) | copy-start | bytes 1572868
  451.4 7.3 %copy-start.7 = (f32[7]{0:T(128)}, f32[7]{0:T(128)S(1)}, u32[]{:S(2)}) copy-start(f32[7]{0:T(128)S(1)} %broadcast_divide_fusion) | copy-start | bytes 88
Sparse Core Ops, SparseCore 0:
  10.1 79.8 all-gather.1
